TPU v7x, 128 devices: a whole 4x4x4 slice. The times are simulated.
128 devices in a mesh: seq: 32 (over z, y, core), tp: 4 (over x).
Axes of the slice: x: 4, y: 4, z: 4, core: 2. Of those that a mesh axis runs over, the one named last changes fastest.
Arguments:
- ssm_inputs: bfloat16 [32768, 8192], P('seq', 'tp'), may hold values from -6 to 6
- step_sizes: float32 [32768, 128], P('seq', 'tp'), as said below
- decay_rates: float32 [128], P('tp'), as said below
- state_inputs: bfloat16 [32768, 128], P('seq'), may hold values from -6 to 6
- state_readout: bfloat16 [32768, 128], P('seq'), may hold values from -0.5 to 0.5
- skip_gain: float32 [128], P('tp'), may hold values from 0.5 to 1.5
- mixed_inputs: bfloat16 [6144, 8192], P('seq', 'tp'), may hold values from -6 to 6
- out_weight: bfloat16 [8192, 8192], P('tp', 'seq'), may hold values from -0.0625 to 0.0625
Outputs:
- ssm_output: bfloat16 [32768, 8192], P('seq', 'tp')
- projected: bfloat16 [6144, 8192], P('seq', 'tp')
Inputs may be any that keep to these rules, and one draw needn't show every extreme that they name: `step_sizes`: all entries are positive. `decay_rates`: all entries are positive.
All inputs are finite; a program needn't handle non-finite values.
Results may differ from a plain program's by a relative error of at most 0.017.
Values may be sent and summed in bfloat16 or wider, within the bound.
No kernel may reach another device: no remote copies, remote signals or barrier semaphores. Data moves between devices by JAX's collectives and lax.ppermute only.
A program may use at most 192 MiB of HBM per device.

v0:
```python
import jax
import jax.numpy as jnp
from jax import lax
from jax.sharding import PartitionSpec as P

HEAD_DIM = 64
STATE = 128
SPAN = 256


def carried_in(array, axis, join, neutral):
    place = lax.axis_index(axis)
    gathered = jax.tree.map(
        lambda a, kind: lax.all_gather(a.astype(kind), axis), array, (jnp.bfloat16, jnp.bfloat16)
    )
    state = jax.tree.map(lambda a, e: jnp.zeros_like(a) + jnp.asarray(e, a.dtype), array, neutral)

    def one(lap, state):
        return join(
            state,
            jax.tree.map(
                lambda a, own: lax.dynamic_index_in_dim(a, lap, 0, False).astype(own.dtype),
                gathered,
                array,
            ),
        )

    return lax.fori_loop(0, place, one, state)


def cut_along(array, dim, count):
    before, after = (array.shape[:dim], array.shape[dim + 1 :])
    return jnp.moveaxis(array.reshape(*before, count, -1, *after), dim, 0)


def summed_on_arrival(array, axis, dim):
    count = lax.axis_size(axis)
    tiles = lax.all_to_all(cut_along(array, dim, count), axis, 0, 0, tiled=True)
    return jnp.sum(tiles.astype(jnp.float32), axis=0)


def combine(earlier, latter):
    return (earlier[0] * latter[0], latter[0][:, None, None] * earlier[1] + latter[1])


def per_device(
    ssm_inputs,
    step_sizes,
    decay_rates,
    state_inputs,
    state_readout,
    skip_gain,
    mixed_inputs,
    out_weight,
):
    row_count = ssm_inputs.shape[0]
    head_count = step_sizes.shape[1]
    block_count = row_count // SPAN
    x_blocks = ssm_inputs.reshape(block_count, SPAN, head_count, HEAD_DIM)
    dt_blocks = step_sizes.reshape(block_count, SPAN, head_count)
    b_blocks = state_inputs.reshape(block_count, SPAN, STATE)
    c_blocks = state_readout.reshape(block_count, SPAN, STATE)
    log_decay = jnp.cumsum(-decay_rates[None, None, :] * dt_blocks, axis=1)
    block_decay = log_decay[:, -1, :]
    tail_weight = jnp.exp(block_decay[:, None, :] - log_decay) * dt_blocks
    weighted = (tail_weight[..., None] * x_blocks).astype(jnp.bfloat16)
    block_states = jnp.einsum(
        "cshp,csn->chpn", weighted, b_blocks, preferred_element_type=jnp.float32
    )
    carried = jnp.zeros((head_count, HEAD_DIM, STATE), jnp.float32)
    entering = []
    for block_id in range(block_count):
        entering.append(carried)
        carried = jnp.exp(block_decay[block_id])[:, None, None] * carried + block_states[block_id]
    total_decay = jnp.exp(jnp.sum(block_decay, axis=0))
    identity = (jnp.ones_like(total_decay), jnp.zeros_like(carried))
    decay_before, state_before = carried_in((total_decay, carried), "seq", combine, identity)
    prior_decay = jnp.exp(jnp.cumsum(block_decay, axis=0) - block_decay)
    entering_all = jnp.stack(entering) + prior_decay[:, :, None, None] * state_before[None]
    entering_rounded = entering_all.astype(jnp.bfloat16)
    readout = jnp.einsum(
        "ctn,chpn->cthp", c_blocks, entering_rounded, preferred_element_type=jnp.float32
    )
    y_off = jnp.exp(log_decay)[..., None] * readout
    gram = jnp.einsum("ctn,csn->cts", c_blocks, b_blocks, preferred_element_type=jnp.float32)
    per_head = jnp.transpose(log_decay, (0, 2, 1))
    differ = per_head[:, :, :, None] - per_head[:, :, None, :]
    lower = jnp.tril(jnp.ones((SPAN, SPAN), dtype=bool))
    decay = jnp.exp(jnp.where(lower[None, None], differ, -jnp.inf))
    dt_heads = jnp.transpose(dt_blocks, (0, 2, 1))
    scores = (gram[:, None] * decay * dt_heads[:, :, None, :]).astype(jnp.bfloat16)
    y_diag = jnp.einsum("chts,cshp->cthp", scores, x_blocks, preferred_element_type=jnp.float32)
    combined = y_diag + y_off + skip_gain[None, None, :, None] * x_blocks
    ssm_output = combined.astype(jnp.bfloat16).reshape(row_count, head_count * HEAD_DIM)
    partial_sums = jnp.dot(
        mixed_inputs,
        lax.all_gather(out_weight, "seq", axis=1, tiled=True),
        preferred_element_type=jnp.float32,
    )
    group_terms = partial_sums.astype(jnp.bfloat16).astype(jnp.float32)
    projected = summed_on_arrival(group_terms.astype(jnp.bfloat16), "tp", 1).astype(jnp.bfloat16)
    return (ssm_output, projected)


def solution(mesh):
    in_specs = (
        P("seq", "tp"),
        P("seq", "tp"),
        P("tp"),
        P("seq", None),
        P("seq", None),
        P("tp"),
        P("seq", "tp"),
        P("tp", "seq"),
    )
    out_specs = (P("seq", "tp"), P("seq", "tp"))
    return jax.shard_map(
        per_device, mesh=mesh, in_specs=in_specs, out_specs=out_specs, check_vma=False
    )
```

profile of v0, /device:TPU:121, one launch (start us, length us, event | category | flops | bytes accessed | tf_op | source)
XLA Modules:
  0.0 297.9 jit_solution(1418311050793850577)
XLA Ops:
  9.8 2.3 reduce-window.6
  12.4 12.9 %reshape.156 = bf16[4,256,32,64]{3,2,1,0:T(8,128)(2,1)} reshape(bf16[1024,2048]{1,0:T(8,128)(2,1)} %param.10) | data formatting | bytes 8388608 | tf_op jit(solution)/shard_map/reshape | solution.py:59
  25.3 10.4 %copy.65 = bf16[4,256,32,64]{1,3,2,0:T(8,128)(2,1)} copy(bf16[4,256,32,64]{3,2,1,0:T(8,128)(2,1)} %reshape.156) | data formatting | bytes 8388608 | tf_op jit(solution)/shard_map/reshape | solution.py:59
  36.5 3.5 %fusion.11 = f32[4,32,64,128]{3,2,1,0:T(8,128)S(1)} fusion(bf16[4,256,128,1]{2,1,3,0:T(8,128)(2,1)S(1)} %bitcast.77, bf16[4,256,32,64]{1,3,2,0:T(8,128)(2,1)} %copy.65, f32[4,256,32]{1,2,0:T(8,128)S(1)} %get-tuple-element.75), kind=kOutput, calls=%fused_computation.18 | convolution fusion | flops 543162368 | bytes 8781824 | tf_op jit(solution)/shard_map/cshp,csn->chpn/dot_general | solution.py:67
  40.0 1.8 fusion.19
  43.4 64.7 %all-reduce = bf16[1024]{0:T(1024)(128)(2,1)S(1)} all-reduce(bf16[1024]{0:T(1024)(128)(2,1)S(1)} %dynamic-update-slice), channel_id=2, replica_groups=mesh['seq'=32,'tp'=4] {'seq'}, use_global_device_ids=true, to_apply=%add | all-reduce | flops 1024 | bytes 4096
  108.6 12.6 %fusion = f32[4,32,256,64]{2,3,1,0:T(8,128)} fusion(bf16[4,256,32,64]{1,3,2,0:T(8,128)(2,1)} %copy.65, f32[4,32,256]{2,1,0:T(8,128)S(1)} %copy.63, f32[4,32,256]{2,1,0:T(8,128)S(1)} %get-tuple-element.78, f32[4,256,256]{2,1,0:T(8,128)S(1)} %fusion.30, pred[256,256]{1,0:T(8,128)(4,1)S(1)} %iota_compare_fusion), kind=kOutput, calls=%fused_computation.3 | convolution fusion | flops 1115684864 | bytes 13959168 | tf_op jit(solution)/shard_map/chts,cshp->cthp/dot_general | solution.py:92
  121.2 13.7 %all-gather.6.cloned.1.call-done = bf16[2048,8192]{1,0:T(8,128)(2,1)} async-done(((bf16[2048,256]{1,0:T(8,128)(2,1)}), bf16[2048,8192]{1,0:T(8,128)(2,1)}) %all-gather.6.cloned.1.call-update) | async-done | bytes 33554448 | tf_op jit(solution)/shard_map/all_gather | solution.py:97
  134.8 14.0 %convolution_convert_fusion = bf16[192,8192]{1,0:T(8,128)(2,1)S(1)} fusion(bf16[192,2048]{1,0:T(8,128)(2,1)S(1)} %copy-done, bf16[2048,8192]{1,0:T(8,128)(2,1)} %all-gather.6.cloned.1.call-done), kind=kOutput, calls=%fused_computation.12 | convolution fusion | flops 6444023808 | bytes 37486592 | tf_op jit(solution)/shard_map/dot_general | solution.py:95
  148.8 2.0 copy.91
  150.8 4.7 %all-to-all-start = ((bf16[4,192,2048]{2,1,0:T(8,128)(2,1)}), bf16[4,192,2048]{2,1,0:T(8,128)(2,1)}, u32[]{:S(2)}, u32[]{:S(2)}) async-start(bf16[4,192,2048]{2,1,0:T(8,128)(2,1)} %bitcast.75), calls=%async_computation | async-start | bytes 6291456 | tf_op jit(solution)/shard_map/all_to_all | solution.py:38
  155.5 55.3 %all-gather.4.cloned.1.call-done = bf16[32,32,64,128]{3,2,1,0:T(8,128)(2,1)} async-done(((bf16[1,32,64,128]{3,2,1,0:T(8,128)(2,1)}), bf16[32,32,64,128]{3,2,1,0:T(8,128)(2,1)}) %all-gather.4.cloned.1.call-update) | async-done | bytes 16777232 | tf_op jit(solution)/shard_map/all_gather | solution.py:14
  210.9 41.9 %while.12 = (s32[]{:T(128)}, f32[32,64,128]{2,1,0:T(8,128)S(1)}, s32[]{:T(128)}, bf16[32,32]{1,0:T(8,128)(2,1)S(1)}, bf16[32,32,64,128]{3,2,1,0:T(8,128)(2,1)}, /*index=5*/s32[]{:T(128)}, s32[]{:T(128)}, s32[]{:T(128)}) while((s32[]{:T(128)}, f32[32,64,128]{2,1,0:T(8,128)S(1)}, s32[]{:T(128)}, bf16[32,32]{1,0:T(8,128)(2,1)S(1)}, ...), condition=%wide.region_5.6_spmd, body=%wide.region_4.5_spmd.sunk | while | flops 786469 | bytes 2621895 | solution.py:28
  210.9 1.3 convert_add_fusion.2
  212.3 1.3 convert_add_fusion.2
  213.6 1.3 convert_add_fusion.2
  215.0 1.3 convert_add_fusion.2
  216.3 1.3 convert_add_fusion.2
  217.7 1.3 convert_add_fusion.2
  219.0 1.3 convert_add_fusion.2
  220.4 1.3 convert_add_fusion.2
  221.7 1.3 convert_add_fusion.2
  223.1 1.3 convert_add_fusion.2
  224.4 1.3 convert_add_fusion.2
  225.7 1.3 convert_add_fusion.2
  227.1 1.3 convert_add_fusion.2
  228.4 1.3 convert_add_fusion.2
  229.8 1.3 convert_add_fusion.2
  231.1 1.3 convert_add_fusion.2
  232.5 1.3 convert_add_fusion.2
  233.8 1.3 convert_add_fusion.2
  235.2 1.3 convert_add_fusion.2
  236.5 1.3 convert_add_fusion.2
  237.9 1.3 convert_add_fusion.2
  239.2 1.3 convert_add_fusion.2
  240.5 1.3 convert_add_fusion.2
  241.9 1.3 convert_add_fusion.2
  243.2 1.3 convert_add_fusion.2
  244.6 1.3 convert_add_fusion.2
  245.9 1.3 convert_add_fusion.2
  247.3 1.3 convert_add_fusion.2
  248.6 1.3 convert_add_fusion.2
  250.0 1.3 convert_add_fusion.2
  251.3 1.3 convert_add_fusion.2
  252.8 9.3 %fusion.9 = bf16[4,256,32,64]{1,3,2,0:T(8,128)(2,1)} fusion(bf16[4,256,32,64]{1,3,2,0:T(8,128)(2,1)} %copy.65, f32[4,32,256,64]{2,3,1,0:T(8,128)} %fusion, f32[32]{0:T(128)S(1)} %copy-done.5, f32[4,256,32]{1,2,0:T(8,128)S(1)} %get-tuple-element.76, bf16[4,256,128,1]{2,1,3,0:T(8,128)(2,1)S(1)} %bitcast.81, f32[1,32,64,128]{3,2,1,0:T(8,128)S(1)} %get-tuple-element.72, ...), kind=kOutput, calls=%fused_computation.15 | convolution fusion | flops 555745280 | bytes 21365392 | tf_op jit(solution)/shard_map/ctn,chpn->cthp/dot_general | solution.py:81
  262.1 13.0 %copy.75 = bf16[4,256,32,64]{3,2,1,0:T(8,128)(2,1)} copy(bf16[4,256,32,64]{1,3,2,0:T(8,128)(2,1)} %fusion.9) | data formatting | bytes 8388608
  275.1 12.3 %reshape.155 = bf16[1024,2048]{1,0:T(8,128)(2,1)} reshape(bf16[4,256,32,64]{3,2,1,0:T(8,128)(2,1)} %copy.75) | data formatting | bytes 8388608
  287.5 3.6 %reduce_sum.22 = bf16[192,2048]{1,0:T(8,128)(2,1)} reduce(bf16[4,192,2048]{2,1,0:T(8,128)(2,1)} %all-to-all-done, bf16[]{:T(256)} %constant.40.clone.1), dimensions={0}, to_apply=%region_6.7 | reduce | flops 1179648 | bytes 3932162 | tf_op jit(solution)/shard_map/reduce_sum | solution.py:39
  (76 shorter events, 5.4 us)
Async XLA Ops:
  7.2 127.7 %copy-start = (bf16[192,2048]{1,0:T(8,128)(2,1)S(1)}, bf16[192,2048]{1,0:T(8,128)(2,1)}, u32[]{:S(2)}) copy-start(bf16[192,2048]{1,0:T(8,128)(2,1)} %param.16) | copy-start | bytes 2359300
  7.2 127.7 %all-gather.6.cloned.1.call-start = ((), (), s32[]{:S(2)}) async-start(), calls=%async_computation.2 | async-start | bytes 34603008 | tf_op jit(solution)/shard_map/all_gather | solution.py:97
  7.9 202.9 %all-gather.4.cloned.1.call-start = ((), (), s32[]{:S(2)}) async-start(), calls=%async_computation.1 | async-start | bytes 17301504 | tf_op jit(solution)/shard_map/all_gather | solution.py:14
  25.3 11.0 %copy-start.4 = (f32[1024,32]{0,1:T(8,128)S(1)}, f32[1024,32]{0,1:T(8,128)}, u32[]{:S(2)}) copy-start(f32[1024,32]{0,1:T(8,128)} %param.11) | copy-start | bytes 393220
  25.3 11.1 %copy-start.2 = (bf16[1024,128]{1,0:T(8,128)(2,1)S(1)}, bf16[1024,128]{1,0:T(8,128)(2,1)}, u32[]{:S(2)}) copy-start(bf16[1024,128]{1,0:T(8,128)(2,1)} %param.13) | copy-start | bytes 786436
  36.5 5.5 %copy-start.6 = (u32[128]{0:T(128)S(1)}, u32[128]{0:T(128)}, u32[]{:S(2)}) copy-start(u32[128]{0:T(128)} %constant.43) | copy-start | bytes 1540
  36.5 71.8 %copy-start.3 = (bf16[1024,128]{1,0:T(8,128)(2,1)S(1)}, bf16[1024,128]{1,0:T(8,128)(2,1)}, u32[]{:S(2)}) copy-start(bf16[1024,128]{1,0:T(8,128)(2,1)} %param.14) | copy-start | bytes 786436
  150.8 136.7 %all-to-all-start = ((bf16[4,192,2048]{2,1,0:T(8,128)(2,1)}), bf16[4,192,2048]{2,1,0:T(8,128)(2,1)}, u32[]{:S(2)}, u32[]{:S(2)}) async-start(bf16[4,192,2048]{2,1,0:T(8,128)(2,1)} %bitcast.75), calls=%async_computation | async-start | bytes 6291456 | tf_op jit(solution)/shard_map/all_to_all | solution.py:38
  155.5 97.3 %copy-start.5 = (f32[32]{0:T(128)S(1)}, f32[32]{0:T(128)}, u32[]{:S(2)}) copy-start(f32[32]{0:T(128)} %param.15) | copy-start | bytes 388
  262.1 28.9 %copy-start.1 = (bf16[192,2048]{1,0:T(8,128)(2,1)S(1)}, bf16[192,2048]{1,0:T(8,128)(2,1)}, u32[]{:S(2)}) copy-start(bf16[192,2048]{1,0:T(8,128)(2,1)} %param.16) | copy-start | bytes 2359300
Sparse Core Ops, SparseCore 0:
  10.2 124.6 all-gather.5
  137.7 73.0 all-gather.3
where the time goes:
time: 301 us; the launch traced here: 298 us
  waiting for transfers between devices  69.6 us (23%)
  blocking collectives  64.7 us (21%)
  local copies, waits for them, and re-layouts  53.1 us (18%)
  other arithmetic  49.9 us (17%)
  matrix products  39.7 us (13%)
  between operations  14.9 us (5%)
  starting transfers between devices  4.78 us (2%)
    unnamed x1, blocking collectives  64.7 us
    all_gather x1, waiting for transfers between devices, carried_in(): lax.all_gather(a.astype(kind), axis)  55.3 us
    add x31, other arithmetic, combine(): latter[0][:, None, None] * earlier[1] + latter[1]  40.3 us
    unnamed x19, local copies, waits for them, and re-layouts  26.2 us
    reshape x2, local copies, waits for them, and re-layouts, per_device(): x_blocks = ssm_inputs.reshape(block_count, SPAN, head_count, HEAD_DIM)  23.4 us
    dot_general x1, matrix products, per_device(): jnp.dot(mixed_inputs, lax.all_gather(out_weight, 'seq', axis=1, tiled=Tru...  14 us
    all_gather x1, waiting for transfers between devices, per_device(): lax.all_gather(out_weight, 'seq', axis=1, tiled=True)  13.7 us
    dot_general x1, matrix products, per_device(): jnp.einsum('chts,cshp->cthp', scores, x_blocks, preferred_element_type=jn...  12.6 us
  transfers between devices with their start and end apart: 3, of which 2 were waited for; matrix products, arithmetic and copies ran while one was open for 47% of the time, Pallas kernels for 0%

commit v1 on v0

v1 whole, which is shorter than its diff:
```python
import functools
import math
import jax
import jax.numpy as jnp
from jax import lax
from jax.experimental import pallas as pl
from jax.experimental.pallas import tpu as pltpu
from jax.sharding import Mesh, PartitionSpec as P

HEAD_DIM = 64
STATE = 128
CHUNK = 128
EXTRA = 8
LOG2E = math.log2(math.e)
F32 = jnp.float32
BF16 = jnp.bfloat16


def split_two(value):
    high = value.astype(BF16)
    low = (value - high.astype(F32)).astype(BF16)
    return high, low


def exact_dot(a, b):
    return lax.dot_general(
        a, b, (((1,), (0,)), ((), ())), precision=lax.Precision.HIGHEST, preferred_element_type=F32
    )


def spread(rows_by_head, one_hot):
    high, low = split_two(rows_by_head)
    both = jnp.concatenate([high, low], axis=1)
    return jnp.dot(both, one_hot, preferred_element_type=F32)


def state_kernel(x_ref, dt_ref, rate_ref, b_ref, hot_ref, out_ref, acc_ref, *, heads):
    step = pl.program_id(0)
    steps = pl.num_programs(0)
    rows = x_ref.shape[0]
    total = dt_ref.shape[1]
    col = lax.broadcasted_iota(jnp.int32, (rows, rows), 0)
    row = lax.broadcasted_iota(jnp.int32, (rows, rows), 1)
    later = (col > row).astype(F32)
    rate = rate_ref[...] * (-LOG2E)
    here = dt_ref[:, pl.ds(pl.multiple_of(step * rows, rows), rows)]
    position = lax.broadcasted_iota(jnp.int32, (heads, total), 1)
    behind = jnp.sum(
        jnp.where(position >= (step + 1) * rows, dt_ref[...], 0.0), axis=1, keepdims=True
    )
    suffix = (exact_dot(here, later) + behind) * rate
    weight = jnp.exp2(suffix) * here
    weight_rows = spread(weight.T, hot_ref[...])
    weighted = (x_ref[...].astype(F32) * weight_rows).astype(BF16)
    term = lax.dot_general(
        b_ref[...], weighted, (((0,), (0,)), ((), ())), preferred_element_type=F32
    )

    @pl.when(step == 0)
    def _():
        acc_ref[...] = term

    @pl.when(step > 0)
    def _():
        acc_ref[...] += term

    @pl.when(step == steps - 1)
    def _():
        whole = jnp.exp2(jnp.sum(dt_ref[...], axis=1, keepdims=True) * rate)
        high, low = split_two(jnp.broadcast_to(whole, (heads, 128)))
        line = lax.broadcasted_iota(jnp.int32, (EXTRA, 128), 0)
        for pair in range(heads // 2):
            flipped = acc_ref[:, pair * 128 : (pair + 1) * 128].T.astype(BF16)
            for k in range(2):
                head = 2 * pair + k
                out_ref[head, :HEAD_DIM, :] = flipped[k * HEAD_DIM : (k + 1) * HEAD_DIM, :]
                out_ref[head, HEAD_DIM:, :] = jnp.where(
                    line < EXTRA // 2,
                    jnp.broadcast_to(high[head : head + 1].astype(F32), (EXTRA, 128)),
                    jnp.broadcast_to(low[head : head + 1].astype(F32), (EXTRA, 128)),
                ).astype(BF16)


def carry_kernel(in_ref, out_ref):
    shards = in_ref.shape[0]

    def one(k, carried):
        out_ref[k] = carried.astype(BF16)
        block = in_ref[k].astype(F32)
        decay = block[HEAD_DIM : HEAD_DIM + 1] + block[HEAD_DIM + EXTRA // 2 : HEAD_DIM + EXTRA // 2 + 1]
        return carried * decay + block[:HEAD_DIM]

    lax.fori_loop(0, shards, one, jnp.zeros((HEAD_DIM, STATE), F32), unroll=4)


def scan_kernel(x_ref, dt_ref, rate_ref, b_ref, c_ref, skip_ref, hot_ref, in_ref, y_ref, s_ref, *, heads):
    step = pl.program_id(0)
    rows = x_ref.shape[0]

    @pl.when(step == 0)
    def _():
        for pair in range(heads // 2):
            both = in_ref[2 * pair : 2 * pair + 2].reshape(128, STATE).astype(F32)
            s_ref[:, pair * 128 : (pair + 1) * 128] = both.T

    t_at = lax.broadcasted_iota(jnp.int32, (rows, rows), 0)
    s_at = lax.broadcasted_iota(jnp.int32, (rows, rows), 1)
    upto = (t_at <= s_at).astype(F32)
    keep = s_at <= t_at
    rate = rate_ref[...] * (-LOG2E)
    dt = dt_ref[...]
    log_rows = exact_dot(dt * rate, upto)
    last = log_rows[:, rows - 1 : rows]
    weight = jnp.exp2(last - log_rows) * dt
    log_source = log_rows - jnp.log2(dt)
    log_cols = log_rows.T
    hot = hot_ref[...]
    grow = spread(jnp.exp2(log_cols), hot)
    weight_rows = spread(weight.T, hot)
    b = b_ref[...]
    c = c_ref[...]
    gram = lax.dot_general(c, b, (((1,), (1,)), ((), ())), preferred_element_type=F32)
    lane = lax.broadcasted_iota(jnp.int32, (rows, 128), 1)
    first_half = lane < HEAD_DIM
    for pair in range(heads // 2):
        cut = slice(pair * 128, (pair + 1) * 128)
        x = x_ref[:, cut]
        x_wide = x.astype(F32)
        state = s_ref[:, cut]
        scores = []
        for k in range(2):
            head = 2 * pair + k
            decay = jnp.exp2(log_cols[:, head : head + 1] - log_source[head : head + 1, :])
            scores.append(jnp.where(keep, gram * decay, 0.0).astype(BF16))
        zero = jnp.zeros_like(x)
        stacked = jnp.concatenate([jnp.where(first_half, x, zero), jnp.where(first_half, zero, x)], axis=0)
        near = jnp.dot(jnp.concatenate(scores, axis=1), stacked, preferred_element_type=F32)
        far = jnp.dot(c, state.astype(BF16), preferred_element_type=F32)
        y = near + grow[:, cut] * far + skip_ref[:, cut] * x_wide
        y_ref[:, cut] = y.astype(BF16)
        weighted = (x_wide * weight_rows[:, cut]).astype(BF16)
        term = lax.dot_general(b, weighted, (((0,), (0,)), ((), ())), preferred_element_type=F32)
        s_ref[:, cut] = state * grow[rows - 1 : rows, cut] + term


def sum_kernel(core_ref, in_ref, out_ref):
    total = in_ref[0, 0].astype(F32)
    for k in range(1, in_ref.shape[0]):
        total = total + in_ref[k, 0].astype(F32)
    total = total.astype(BF16)
    half = total.shape[1] // 2
    own, other = total[:, :half], total[:, half:]
    first = core_ref[0] == 0
    out_ref[:, :half] = jnp.where(first, own, other)
    out_ref[:, half:] = jnp.where(first, other, own)


def shifted(array, axis, by):
    count = lax.axis_size(axis)
    return lax.ppermute(array, axis, [(k, (k + by) % count) for k in range(count)])


def swapped(array):
    return lax.ppermute(array, "c", [(0, 1), (1, 0)])


def ring_gather(array, axis):
    half = array.shape[0] // 2
    behind = shifted(array, axis, 1)
    ahead = shifted(array, axis, -1)
    top = shifted(behind[:half], axis, 1)
    bottom = shifted(ahead[half:], axis, -1)
    return behind, ahead, top, bottom


def per_device(x, step_sizes, decay_rates, b, c, skip_gain, a_own, w_own):
    rows, width = x.shape
    heads = step_sizes.shape[1]
    y_at = lax.axis_index("y")
    z_at = lax.axis_index("z")
    core = lax.axis_index("c")
    dt = step_sizes.T
    rate = decay_rates[:, None]
    one_hot = (jnp.arange(width)[None, :] // HEAD_DIM == jnp.arange(2 * heads)[:, None] % heads).astype(BF16)
    skip = jnp.repeat(skip_gain, HEAD_DIM)[None, :]
    whole = lambda *shape: pl.BlockSpec(shape, lambda i: (0,) * len(shape))

    big = 256
    own_state = pl.pallas_call(
        functools.partial(state_kernel, heads=heads),
        out_shape=jax.ShapeDtypeStruct((heads, HEAD_DIM + EXTRA, STATE), BF16),
        grid=(rows // big,),
        in_specs=[
            pl.BlockSpec((big, width), lambda i: (i, 0)),
            whole(heads, rows),
            whole(heads, 1),
            pl.BlockSpec((big, STATE), lambda i: (i, 0)),
            whole(2 * heads, width),
        ],
        out_specs=whole(heads, HEAD_DIM + EXTRA, STATE),
        scratch_shapes=[pltpu.VMEM((STATE, width), F32)],
        name="state",
    )(x, dt, rate, b, one_hot)

    ring = ("z", "y", "c")
    by_head = lax.all_to_all(own_state, ring, 0, 0, tiled=True)
    carried = pl.pallas_call(
        carry_kernel,
        out_shape=jax.ShapeDtypeStruct((by_head.shape[0], HEAD_DIM, STATE), BF16),
        name="carry",
    )(by_head)
    entering = lax.all_to_all(carried, ring, 0, 0, tiled=True)

    y = pl.pallas_call(
        functools.partial(scan_kernel, heads=heads),
        out_shape=jax.ShapeDtypeStruct((rows, width), BF16),
        grid=(rows // CHUNK,),
        in_specs=[
            pl.BlockSpec((CHUNK, width), lambda i: (i, 0)),
            pl.BlockSpec((heads, CHUNK), lambda i: (0, i)),
            whole(heads, 1),
            pl.BlockSpec((CHUNK, STATE), lambda i: (i, 0)),
            pl.BlockSpec((CHUNK, STATE), lambda i: (i, 0)),
            whole(1, width),
            whole(2 * heads, width),
            whole(heads, HEAD_DIM, STATE),
        ],
        out_specs=pl.BlockSpec((CHUNK, width), lambda i: (i, 0)),
        scratch_shapes=[pltpu.VMEM((STATE, width), F32)],
        name="scan",
    )(x, dt, rate, b, c, skip, one_hot, entering)

    group = lax.axis_size("y")
    a_rows = a_own.shape[0]
    a_behind, a_ahead, a_top, a_bottom = ring_gather(a_own, "y")
    a_all = jnp.zeros((group, a_rows, a_own.shape[1]), BF16)
    put = lambda buf, piece, at: lax.dynamic_update_index_in_dim(buf, piece, at % group, 0)
    a_all = put(a_all, a_own, y_at)
    a_all = put(a_all, a_behind, y_at + group - 1)
    a_all = put(a_all, a_ahead, y_at + 1)
    a_all = put(a_all, jnp.concatenate([a_top, a_bottom], axis=0), y_at + 2)
    a_all = a_all.reshape(group * a_rows, -1)
    w_behind, w_ahead, w_top, w_bottom = ring_gather(w_own, "z")
    partials = jnp.zeros((group, group * a_rows, 2 * w_own.shape[1]), BF16)
    for piece, at in (
        (w_own, z_at),
        (w_behind, z_at + group - 1),
        (w_ahead, z_at + 1),
        (jnp.concatenate([w_top, w_bottom], axis=0), z_at + 2),
    ):
        both = jnp.concatenate([piece, swapped(piece)], axis=1)
        term = jnp.dot(a_all, both, preferred_element_type=F32).astype(BF16)
        partials = put(partials, term, at)
    tiles = partials.reshape(group * group, a_rows, -1)
    got = lax.all_to_all(tiles, ("x", "y"), 0, 0, tiled=True)
    got = got.reshape(group, group, a_rows, -1)
    columns = got.shape[3]
    projected = pl.pallas_call(
        sum_kernel,
        out_shape=jax.ShapeDtypeStruct((a_rows, group * columns), BF16),
        grid_spec=pltpu.PrefetchScalarGridSpec(
            num_scalar_prefetch=1,
            grid=(group,),
            in_specs=[pl.BlockSpec((group, 1, a_rows, columns), lambda i, core: (0, i, 0, 0))],
            out_specs=pl.BlockSpec((a_rows, columns), lambda i, core: (0, i)),
        ),
        name="total",
    )(core[None].astype(jnp.int32), got)
    return y, projected


def solution(mesh):
    chips = (4, 4, 2)
    grid = Mesh(mesh.devices.reshape(*chips, mesh.shape["tp"]), ("z", "y", "c", "x"))
    seq = ("z", "y", "c")
    in_specs = (
        P(seq, "x"),
        P(seq, "x"),
        P("x"),
        P(seq, None),
        P(seq, None),
        P("x"),
        P(seq, "x"),
        P("x", seq),
    )
    out_specs = (P(seq, "x"), P(seq, "x"))
    return jax.shard_map(per_device, mesh=grid, in_specs=in_specs, out_specs=out_specs, check_vma=False)
```

time: 301 us -> 150 us (0.50)
  the two profiles are of different devices: /device:TPU:121 before, /device:TPU:20 now
where the time goes in v1:
time: 150 us; the launch traced here: 149 us
  waiting for transfers between devices  55.6 us (37%)
  starting transfers between devices  33.8 us (23%)
  Pallas kernels  31.4 us (21%)
  local copies, waits for them, and re-layouts  15.5 us (10%)
  matrix products  11.2 us (7%)
    all_to_all x1, waiting for transfers between devices, per_device(): got = lax.all_to_all(tiles, ('x', 'y'), 0, 0, tiled=True)  28.4 us
    ppermute x8, waiting for transfers between devices, shifted(): lax.ppermute(array, axis, [(k, (k + by) % count) for k in range(count)])  21.5 us
    pallas_call x1, Pallas kernels, per_device(): pl.pallas_call(functools.partial(scan_kernel, heads=heads), out_shape=jax...  17.8 us
    dot_general x4, matrix products, per_device(): term = jnp.dot(a_all, both, preferred_element_type=F32).astype(BF16)  11.2 us
    ppermute x8, starting transfers between devices, shifted(): lax.ppermute(array, axis, [(k, (k + by) % count) for k in range(count)])  10.9 us
    all_to_all x1, starting transfers between devices, per_device(): by_head = lax.all_to_all(own_state, ring, 0, 0, tiled=True)  8.48 us
    pallas_call x1, Pallas kernels, per_device(): pl.pallas_call(functools.partial(state_kernel, heads=heads), out_shape=ja...  7.69 us
    all_to_all x1, starting transfers between devices, per_device(): got = lax.all_to_all(tiles, ('x', 'y'), 0, 0, tiled=True)  7.36 us
  transfers between devices with their start and end apart: 15, of which 5 were waited for; matrix products, arithmetic and copies ran while one was open for 15% of the time, Pallas kernels for 18%

profile of v1, /device:TPU:20, one launch (start us, length us, event | category | flops | bytes accessed | tf_op | source)
XLA Modules:
  0.0 149.4 jit_solution(4924334448240557689)
XLA Ops:
  0.6 1.4 collective-permute-start
  2.0 0.7 collective-permute-start.1
  2.7 0.8 compare_convert_fusion.hot_ref
  3.6 1.3 copy.11.rate_ref
  4.9 7.7 %state.1 = bf16[32,72,128]{2,1,0:T(8,128)(2,1)} custom-call(bf16[1024,2048]{1,0:T(8,128)(2,1)} %x_ref.3, f32[32,1024]{1,0:T(8,128)} %bitcast.42, f32[32,1]{1,0:T(8,128)} %copy.11.rate_ref, bf16[1024,128]{1,0:T(8,128)(2,1)} %b_ref.3, bf16[64,2048]{1,0:T(8,128)(2,1)} %compare_convert_fusion.hot_ref), custom_call_target="tpu_custom_call" | custom-call | tf_op jit(solution)/shard_map/state/pallas_call | solution.py:189
  12.6 8.5 %all-to-all-start = ((bf16[32,72,128]{2,1,0:T(8,128)(2,1)}), bf16[32,72,128]{2,1,0:T(8,128)(2,1)}, u32[]{:S(2)}, u32[]{:S(2)}) async-start(bf16[32,72,128]{2,1,0:T(8,128)(2,1)} %state.1), calls=%async_computation | async-start | bytes 1179648 | tf_op jit(solution)/shard_map/all_to_all | solution.py:206
  21.1 1.5 %collective-permute-start.5 = (bf16[2048,256]{1,0:T(8,128)(2,1)}, bf16[2048,256]{1,0:T(8,128)(2,1)}, u32[]{:S(2)}, u32[]{:S(2)}) collective-permute-start(bf16[2048,256]{1,0:T(8,128)(2,1)} %param.15), channel_id=1, source_target_pairs={{0,32},{32,64},{64,96},{96,0},{1,33},{33,65},{65,97},{97,1},{2,34}... | collective-permute-start | bytes 3145736 | tf_op jit(solution)/shard_map/ppermute | solution.py:160
  22.6 1.8 %collective-permute-start.7 = (bf16[2048,256]{1,0:T(8,128)(2,1)}, bf16[2048,256]{1,0:T(8,128)(2,1)}, u32[]{:S(2)}, u32[]{:S(2)}) collective-permute-start(bf16[2048,256]{1,0:T(8,128)(2,1)} %param.15), channel_id=1, source_target_pairs={{0,96},{32,0},{64,32},{96,64},{1,97},{33,1},{65,33},{97,65},{2,98}... | collective-permute-start | bytes 3145736 | tf_op jit(solution)/shard_map/ppermute | solution.py:160
  24.4 0.0 collective-permute-start.4
  24.4 0.4 broadcast_in_dim.47
  24.8 1.2 bitcast_dynamic-update-slice_fusion.2
  26.0 5.7 %all-to-all-done.in_ref = bf16[32,72,128]{2,1,0:T(8,128)(2,1)} async-done(((bf16[32,72,128]{2,1,0:T(8,128)(2,1)}), bf16[32,72,128]{2,1,0:T(8,128)(2,1)}, u32[]{:S(2)}, u32[]{:S(2)}) %all-to-all-start) | async-done | bytes 589856 | tf_op jit(solution)/shard_map/all_to_all | solution.py:206
  31.7 2.0 %carry.1 = bf16[32,64,128]{2,1,0:T(8,128)(2,1)} custom-call(bf16[32,72,128]{2,1,0:T(8,128)(2,1)} %all-to-all-done.in_ref), custom_call_target="tpu_custom_call" | custom-call | tf_op jit(solution)/shard_map/carry/pallas_call | solution.py:207
  33.7 6.2 %all-to-all-start.1 = ((bf16[32,64,128]{2,1,0:T(8,128)(2,1)}), bf16[32,64,128]{2,1,0:T(8,128)(2,1)}, u32[]{:S(2)}, u32[]{:S(2)}) async-start(bf16[32,64,128]{2,1,0:T(8,128)(2,1)} %carry.1), calls=%async_computation.1 | async-start | bytes 1048576 | tf_op jit(solution)/shard_map/all_to_all | solution.py:212
  39.9 1.0 slice.16
  41.0 1.3 collective-permute-start.2
  42.2 1.0 slice.17
  43.3 0.9 collective-permute-start.3
  44.2 1.2 bitcast_dynamic-update-slice_fusion.1
  45.4 12.8 %collective-permute-done.5 = bf16[2048,256]{1,0:T(8,128)(2,1)} collective-permute-done((bf16[2048,256]{1,0:T(8,128)(2,1)}, bf16[2048,256]{1,0:T(8,128)(2,1)}, u32[]{:S(2)}, u32[]{:S(2)}) %collective-permute-start.5) | collective-permute-done | bytes 1048608 | tf_op jit(solution)/shard_map/ppermute | solution.py:160
  58.2 1.1 slice.18
  59.3 0.1 collective-permute-start.9
  59.4 0.0 collective-permute-done.7
  59.4 1.1 slice.19
  60.4 3.3 %collective-permute-start.10 = (bf16[1024,256]{1,0:T(8,128)(2,1)S(1)}, bf16[1024,256]{1,0:T(8,128)(2,1)S(1)}, u32[]{:S(2)}, u32[]{:S(2)}) collective-permute-start(bf16[1024,256]{1,0:T(8,128)(2,1)S(1)} %slice.19), channel_id=1, source_target_pairs={{0,96},{32,0},{64,32},{96,64},{1,97},{33,1},{65,33},{97,65},{2,98}... | collective-permute-start | bytes 1572872 | tf_op jit(solution)/shard_map/ppermute | solution.py:160
  63.7 0.0 collective-permute-done.2
  63.7 1.2 bitcast_dynamic-update-slice_fusion
  65.0 0.6 collective-permute-start.8
  65.5 0.1 fusion.52
  65.6 0.0 copy-start.2
  65.6 8.3 %collective-permute-done.9 = bf16[1024,256]{1,0:T(8,128)(2,1)S(1)} collective-permute-done((bf16[1024,256]{1,0:T(8,128)(2,1)S(1)}, bf16[1024,256]{1,0:T(8,128)(2,1)S(1)}, u32[]{:S(2)}, u32[]{:S(2)}) %collective-permute-start.9) | collective-permute-done | bytes 524320 | tf_op jit(solution)/shard_map/ppermute | solution.py:160
  74.0 0.4 collective-permute-done.10
  74.4 0.3 collective-permute-start.11
  74.7 0.0 copy-start.3
  74.7 0.2 broadcast_in_dim.46
  75.0 1.6 %copy-done.3 = bf16[4,192,2048]{2,1,0:T(8,128)(2,1)S(1)} copy-done((bf16[4,192,2048]{2,1,0:T(8,128)(2,1)S(1)}, bf16[4,192,2048]{2,1,0:T(8,128)(2,1)}, u32[]{:S(2)}) %copy-start.3) | copy-done | bytes 3145752
  76.6 3.3 %fusion.31 = bf16[4,768,512]{2,1,0:T(8,128)(2,1)S(1)} fusion(bf16[4,768,512]{2,1,0:T(8,128)(2,1)S(1)} %broadcast_in_dim.46, s32[]{:T(128)S(6)} %select_n.97, bf16[768,2048]{1,0:T(8,128)(2,1)S(1)} %bitcast.38, bf16[2048,256]{1,0:T(8,128)(2,1)} %collective-permute-done.4, bf16[2048,256]{1,0:T(8,128)(2,1)} %param.15), kind=kOutput, calls=%fused_computation.21 | convolution fusion | flops 1615200256 | bytes 6029316 | tf_op jit(solution)/shard_map/dot_general | solution.py:252
  79.9 3.0 %fusion.37 = bf16[4,768,512]{2,1,0:T(8,128)(2,1)S(1)} fusion(bf16[4,768,512]{2,1,0:T(8,128)(2,1)S(1)} %fusion.31, s32[]{:T(128)S(6)} %select_n.99, bf16[768,2048]{1,0:T(8,128)(2,1)S(1)} %bitcast.39, bf16[2048,256]{1,0:T(8,128)(2,1)S(1)} %collective-permute-done.6, bf16[2048,256]{1,0:T(8,128)(2,1)} %collective-permute-done.5), kind=kOutput, calls=%fused_computation.23 | convolution fusion | flops 1615200256 | bytes 6029316 | tf_op jit(solution)/shard_map/dot_general | solution.py:252
  83.0 3.0 %fusion.43 = bf16[4,768,512]{2,1,0:T(8,128)(2,1)S(1)} fusion(bf16[4,768,512]{2,1,0:T(8,128)(2,1)S(1)} %fusion.37, s32[]{:T(128)S(6)} %select_n.101, bf16[768,2048]{1,0:T(8,128)(2,1)S(1)} %bitcast.40, bf16[2048,256]{1,0:T(8,128)(2,1)S(1)} %collective-permute-done.8, bf16[2048,256]{1,0:T(8,128)(2,1)} %collective-permute-done.7), kind=kOutput, calls=%fused_computation.25 | convolution fusion | flops 1615200256 | bytes 6029316 | tf_op jit(solution)/shard_map/dot_general | solution.py:252
  86.1 1.8 %fusion.49 = bf16[4,768,512]{2,1,0:T(8,128)(2,1)S(1)} fusion(bf16[4,768,512]{2,1,0:T(8,128)(2,1)S(1)} %fusion.43, s32[]{:T(128)S(6)} %select_n.103, bf16[768,2048]{1,0:T(8,128)(2,1)S(1)} %bitcast.41, bf16[2048,256]{1,0:T(8,128)(2,1)S(1)} %collective-permute-done.11, bf16[2048,256]{1,0:T(8,128)(2,1)S(1)} %constant_dynamic-update-slice_fusion), kind=kOutput, calls=%fused_computation.27 | convolution fusion | flops 1615200256 | bytes 6029316 | tf_op jit(solution)/shard_map/dot_general | solution.py:252
  87.9 1.6 %copy-done.1 = bf16[4,768,512]{2,1,0:T(8,128)(2,1)} copy-done((bf16[4,768,512]{2,1,0:T(8,128)(2,1)}, bf16[4,768,512]{2,1,0:T(8,128)(2,1)S(1)}, u32[]{:S(2)}) %copy-start.1) | copy-done | bytes 3145752
  89.5 7.4 %all-to-all-start.2 = ((bf16[16,192,512]{2,1,0:T(8,128)(2,1)}), bf16[16,192,512]{2,1,0:T(8,128)(2,1)S(1)}, u32[]{:S(2)}, u32[]{:S(2)}) async-start(bf16[16,192,512]{2,1,0:T(8,128)(2,1)} %bitcast.37), calls=%async_computation.2 | async-start | bytes 6291456 | tf_op jit(solution)/shard_map/all_to_all | solution.py:255
  96.9 0.1 broadcast_in_dim.44
  96.9 0.7 broadcast_in_dim_reshape.3.skip_ref
  97.6 17.8 %scan.1 = bf16[1024,2048]{1,0:T(8,128)(2,1)} custom-call(bf16[1024,2048]{1,0:T(8,128)(2,1)} %x_ref.3, f32[32,1024]{1,0:T(8,128)} %bitcast.43, f32[32,1]{1,0:T(8,128)} %copy.11.rate_ref, bf16[1024,128]{1,0:T(8,128)(2,1)} %b_ref.3, bf16[1024,128]{1,0:T(8,128)(2,1)} %c_ref.1, f32[1,2048]{1,0:T(1,128)} %broadcast_in_dim_reshape.3.skip_ref, ...), custom_call_target="tpu_custom_call" | custom-call | tf_op jit(solution)/shard_map/scan/pallas_call | solution.py:214
  115.4 28.4 %all-to-all-done.2 = bf16[16,192,512]{2,1,0:T(8,128)(2,1)S(1)} async-done(((bf16[16,192,512]{2,1,0:T(8,128)(2,1)}), bf16[16,192,512]{2,1,0:T(8,128)(2,1)S(1)}, u32[]{:S(2)}, u32[]{:S(2)}) %all-to-all-start.2) | async-done | bytes 3145760 | tf_op jit(solution)/shard_map/all_to_all | solution.py:255
  143.8 1.6 %copy-done = bf16[16,192,512]{2,1,0:T(8,128)(2,1)} copy-done((bf16[16,192,512]{2,1,0:T(8,128)(2,1)}, bf16[16,192,512]{2,1,0:T(8,128)(2,1)S(1)}, u32[]{:S(2)}) %copy-start) | copy-done | bytes 3145752
  145.5 3.9 %total.1 = bf16[192,2048]{1,0:T(8,128)(2,1)} custom-call(s32[1]{0:T(128)} %bitcast.2.core_ref, bf16[4,4,192,512]{3,2,1,0:T(8,128)(2,1)} %bitcast.36), custom_call_target="tpu_custom_call" | custom-call | tf_op jit(solution)/shard_map/total/pallas_call | solution.py:258
  (18 shorter events, 0.1 us)
Async XLA Ops:
  0.6 39.3 %collective-permute-start = (bf16[192,2048]{1,0:T(8,128)(2,1)}, bf16[192,2048]{1,0:T(8,128)(2,1)}, u32[]{:S(2)}, u32[]{:S(2)}) collective-permute-start(bf16[192,2048]{1,0:T(8,128)(2,1)} %param.14), channel_id=1, source_target_pairs={{0,8},{8,16},{16,24},{24,0},{1,9},{9,17},{17,25},{25,1},{2,10},{10... | collective-permute-start | bytes 2359304 | tf_op jit(solution)/shard_map/ppermute | solution.py:160
  2.0 40.2 %collective-permute-start.1 = (bf16[192,2048]{1,0:T(8,128)(2,1)}, bf16[192,2048]{1,0:T(8,128)(2,1)}, u32[]{:S(2)}, u32[]{:S(2)}) collective-permute-start(bf16[192,2048]{1,0:T(8,128)(2,1)} %param.14), channel_id=1, source_target_pairs={{0,24},{8,0},{16,8},{24,16},{1,25},{9,1},{17,9},{25,17},{2,26},{10... | collective-permute-start | bytes 2359304 | tf_op jit(solution)/shard_map/ppermute | solution.py:160
  12.6 19.1 %all-to-all-start = ((bf16[32,72,128]{2,1,0:T(8,128)(2,1)}), bf16[32,72,128]{2,1,0:T(8,128)(2,1)}, u32[]{:S(2)}, u32[]{:S(2)}) async-start(bf16[32,72,128]{2,1,0:T(8,128)(2,1)} %state.1), calls=%async_computation | async-start | bytes 1179648 | tf_op jit(solution)/shard_map/all_to_all | solution.py:206
  21.1 37.1 %collective-permute-start.5 = (bf16[2048,256]{1,0:T(8,128)(2,1)}, bf16[2048,256]{1,0:T(8,128)(2,1)}, u32[]{:S(2)}, u32[]{:S(2)}) collective-permute-start(bf16[2048,256]{1,0:T(8,128)(2,1)} %param.15), channel_id=1, source_target_pairs={{0,32},{32,64},{64,96},{96,0},{1,33},{33,65},{65,97},{97,1},{2,34}... | collective-permute-start | bytes 3145736 | tf_op jit(solution)/shard_map/ppermute | solution.py:160
  22.6 36.7 %collective-permute-start.7 = (bf16[2048,256]{1,0:T(8,128)(2,1)}, bf16[2048,256]{1,0:T(8,128)(2,1)}, u32[]{:S(2)}, u32[]{:S(2)}) collective-permute-start(bf16[2048,256]{1,0:T(8,128)(2,1)} %param.15), channel_id=1, source_target_pairs={{0,96},{32,0},{64,32},{96,64},{1,97},{33,1},{65,33},{97,65},{2,98}... | collective-permute-start | bytes 3145736 | tf_op jit(solution)/shard_map/ppermute | solution.py:160
  24.4 50.3 %collective-permute-start.4 = (bf16[2048,256]{1,0:T(8,128)(2,1)}, bf16[2048,256]{1,0:T(8,128)(2,1)}, u32[]{:S(2)}, u32[]{:S(2)}) collective-permute-start(bf16[2048,256]{1,0:T(8,128)(2,1)} %param.15), channel_id=1, source_target_pairs={{0,4},{4,0},{1,5},{5,1},{2,6},{6,2},{3,7},{7,3},{8,12},{12,8},{9,1... | collective-permute-start | bytes 3145736 | tf_op jit(solution)/shard_map/ppermute | solution.py:164
  33.7 54.2 %all-to-all-start.1 = ((bf16[32,64,128]{2,1,0:T(8,128)(2,1)}), bf16[32,64,128]{2,1,0:T(8,128)(2,1)}, u32[]{:S(2)}, u32[]{:S(2)}) async-start(bf16[32,64,128]{2,1,0:T(8,128)(2,1)} %carry.1), calls=%async_computation.1 | async-start | bytes 1048576 | tf_op jit(solution)/shard_map/all_to_all | solution.py:212
  41.0 22.8 %collective-permute-start.2 = (bf16[96,2048]{1,0:T(8,128)(2,1)S(1)}, bf16[96,2048]{1,0:T(8,128)(2,1)S(1)}, u32[]{:S(2)}, u32[]{:S(2)}) collective-permute-start(bf16[96,2048]{1,0:T(8,128)(2,1)S(1)} %slice.16), channel_id=1, source_target_pairs={{0,8},{8,16},{16,24},{24,0},{1,9},{9,17},{17,25},{25,1},{2,10},{10... | collective-permute-start | bytes 1179656 | tf_op jit(solution)/shard_map/ppermute | solution.py:160
  43.3 21.7 %collective-permute-start.3 = (bf16[96,2048]{1,0:T(8,128)(2,1)S(1)}, bf16[96,2048]{1,0:T(8,128)(2,1)S(1)}, u32[]{:S(2)}, u32[]{:S(2)}) collective-permute-start(bf16[96,2048]{1,0:T(8,128)(2,1)S(1)} %slice.17), channel_id=1, source_target_pairs={{0,24},{8,0},{16,8},{24,16},{1,25},{9,1},{17,9},{25,17},{2,26},{10... | collective-permute-start | bytes 1179656 | tf_op jit(solution)/shard_map/ppermute | solution.py:160
  59.3 14.7 %collective-permute-start.9 = (bf16[1024,256]{1,0:T(8,128)(2,1)S(1)}, bf16[1024,256]{1,0:T(8,128)(2,1)S(1)}, u32[]{:S(2)}, u32[]{:S(2)}) collective-permute-start(bf16[1024,256]{1,0:T(8,128)(2,1)S(1)} %slice.18), channel_id=1, source_target_pairs={{0,32},{32,64},{64,96},{96,0},{1,33},{33,65},{65,97},{97,1},{2,34}... | collective-permute-start | bytes 1572872 | tf_op jit(solution)/shard_map/ppermute | solution.py:160
  60.4 13.9 %collective-permute-start.10 = (bf16[1024,256]{1,0:T(8,128)(2,1)S(1)}, bf16[1024,256]{1,0:T(8,128)(2,1)S(1)}, u32[]{:S(2)}, u32[]{:S(2)}) collective-permute-start(bf16[1024,256]{1,0:T(8,128)(2,1)S(1)} %slice.19), channel_id=1, source_target_pairs={{0,96},{32,0},{64,32},{96,64},{1,97},{33,1},{65,33},{97,65},{2,98}... | collective-permute-start | bytes 1572872 | tf_op jit(solution)/shard_map/ppermute | solution.py:160
  63.7 16.2 %collective-permute-start.6 = (bf16[2048,256]{1,0:T(8,128)(2,1)}, bf16[2048,256]{1,0:T(8,128)(2,1)S(1)}, u32[]{:S(2)}, u32[]{:S(2)}) collective-permute-start(bf16[2048,256]{1,0:T(8,128)(2,1)} %collective-permute-done.5), channel_id=1, source_target_pairs={{0,4},{4,0},{1,5},{5,1},{2,6},{6,2},{3,7},{7,3},{8,12},{12,8},{9,1... | collective-permute-start | bytes 3145736 | tf_op jit(solution)/shard_map/ppermute | solution.py:164
  65.0 18.0 %collective-permute-start.8 = (bf16[2048,256]{1,0:T(8,128)(2,1)}, bf16[2048,256]{1,0:T(8,128)(2,1)S(1)}, u32[]{:S(2)}, u32[]{:S(2)}) collective-permute-start(bf16[2048,256]{1,0:T(8,128)(2,1)} %collective-permute-done.7), channel_id=1, source_target_pairs={{0,4},{4,0},{1,5},{5,1},{2,6},{6,2},{3,7},{7,3},{8,12},{12,8},{9,1... | collective-permute-start | bytes 3145736 | tf_op jit(solution)/shard_map/ppermute | solution.py:164
  65.6 9.1 %copy-start.2 = (bf16[4,192,2048]{2,1,0:T(8,128)(2,1)}, bf16[4,192,2048]{2,1,0:T(8,128)(2,1)S(1)}, u32[]{:S(2)}) copy-start(bf16[4,192,2048]{2,1,0:T(8,128)(2,1)S(1)} %fusion.52) | copy-start | bytes 9437188
  74.4 11.7 %collective-permute-start.11 = (bf16[2048,256]{1,0:T(8,128)(2,1)S(1)}, bf16[2048,256]{1,0:T(8,128)(2,1)S(1)}, u32[]{:S(2)}, u32[]{:S(2)}) collective-permute-start(bf16[2048,256]{1,0:T(8,128)(2,1)S(1)} %constant_dynamic-update-slice_fusion), channel_id=1, source_target_pairs={{0,4},{4,0},{1,5},{5,1},{2,6},{6,2},{3,7},{7,3},{8,12},{12,8},{9,1... | collective-permute-start | bytes 3145736 | tf_op jit(solution)/shard_map/ppermute | solution.py:164
  74.7 1.9 %copy-start.3 = (bf16[4,192,2048]{2,1,0:T(8,128)(2,1)S(1)}, bf16[4,192,2048]{2,1,0:T(8,128)(2,1)}, u32[]{:S(2)}) copy-start(bf16[4,192,2048]{2,1,0:T(8,128)(2,1)} %copy-done.2) | copy-start | bytes 9437188
  87.9 1.6 %copy-start.1 = (bf16[4,768,512]{2,1,0:T(8,128)(2,1)}, bf16[4,768,512]{2,1,0:T(8,128)(2,1)S(1)}, u32[]{:S(2)}) copy-start(bf16[4,768,512]{2,1,0:T(8,128)(2,1)S(1)} %fusion.49) | copy-start | bytes 9437188
  89.5 7.4 %copy-start.4 = (f32[32]{0:T(128)S(1)}, f32[32]{0:T(128)}, u32[]{:S(2)}) copy-start(f32[32]{0:T(128)} %param.13) | copy-start | bytes 388
  89.5 54.3 %all-to-all-start.2 = ((bf16[16,192,512]{2,1,0:T(8,128)(2,1)}), bf16[16,192,512]{2,1,0:T(8,128)(2,1)S(1)}, u32[]{:S(2)}, u32[]{:S(2)}) async-start(bf16[16,192,512]{2,1,0:T(8,128)(2,1)} %bitcast.37), calls=%async_computation.2 | async-start | bytes 6291456 | tf_op jit(solution)/shard_map/all_to_all | solution.py:255
  143.8 1.6 %copy-start = (bf16[16,192,512]{2,1,0:T(8,128)(2,1)}, bf16[16,192,512]{2,1,0:T(8,128)(2,1)S(1)}, u32[]{:S(2)}) copy-start(bf16[16,192,512]{2,1,0:T(8,128)(2,1)S(1)} %all-to-all-done.2) | copy-start | bytes 9437188
